TPU v7x, 32 devices: a whole 2x2x4 slice. The times are simulated.
32 devices in a mesh: seq: 8 (over y, x, core), head: 4 (over z).
Axes of the slice: x: 2, y: 2, z: 4, core: 2. Of those that a mesh axis runs over, the one named last changes fastest.
Arguments:
- queries: bfloat16 [1024, 8192], P('seq', 'head'), may hold values from -2.5 to 2.5
- keys: bfloat16 [1024, 8192], P('seq', 'head'), may hold values from -2.5 to 2.5
- values: bfloat16 [1024, 4096], P('seq', 'head'), may hold values from -2.5 to 2.5
- out_grad: bfloat16 [1024, 4096], P('seq', 'head'), may hold values from -2.5 to 2.5
- log_gate: float32 [64, 1024], P('head', 'seq'), may hold values from -1 to 0
- level_weight: float32 [6, 64, 1024], P(None, 'head', 'seq'), may hold values from 0.25 to 2
- doc_start: int32 [1024], P('seq'), may hold values 0 or 1
Outputs:
- grad_queries: bfloat16 [1024, 8192], P('seq', 'head')
- grad_keys: bfloat16 [1024, 8192], P('seq', 'head')
- grad_values: bfloat16 [1024, 4096], P('seq', 'head')
- grad_level_weight: float32 [6, 64, 1024], P(None, 'head', 'seq')
- grad_log_gate: float32 [64, 1024], P('head', 'seq')
All inputs are finite; a program needn't handle non-finite values. No bound on the sum of `doc_start` on one device may be relied on, other than what follows from the above.
Results may differ from a plain program's by a relative error of at most 0.0027.
Values sent between devices are 32-bit elements; how exact they have to be, the bound alone decides.
A program may use at most 128 MiB of HBM per device.

v0:
```python
import functools

import jax
import jax.numpy as jnp
from jax import lax
from jax.experimental import pallas as pl
from jax.experimental.pallas import tpu as pltpu
from jax.sharding import PartitionSpec as P

SPAN = 64
F32 = jnp.float32
BF16 = jnp.bfloat16
NN = (((1,), (0,)), ((), ()))
NT = (((1,), (1,)), ((), ()))
TN = (((0,), (0,)), ((), ()))
MESH = pl.DeviceIdType.MESH


def dot(a, b, dims):
    return lax.dot_general(a, b, dims, preferred_element_type=F32)


def split(x):
    high = x.astype(BF16)
    return high, (x - high.astype(F32)).astype(BF16)


def dot_fine(x, b, dims):
    high, low = split(x)
    return dot(high, b, dims) + dot(low, b, dims)


def span_level(a, b, levels):
    return 0 if a == b else min(levels - 1, (a ^ b).bit_length())


def kernel(
    seq_count,
    head_count,
    q_ref,
    k_ref,
    v_ref,
    g_ref,
    lg_ref,
    lw_ref,
    ds_ref,
    gq_ref,
    gk_ref,
    gv_ref,
    gl_ref,
    gg_ref,
    cum_s,
    col_s,
    lead_s,
    tail_s,
    bias_s,
    vt_s,
    gt_s,
    vg_s,
    gq_s,
    gk_s,
    drift_s,
    coef_s,
    state_s,
    back_s,
    lvl,
    got_s,
    got_u,
    sum_s,
    sum_u,
    dec,
    got_dec,
    tot,
    sq,
    lvl_send,
    lvl_recv,
    fwd_send,
    fwd_recv,
    s_send,
    s_recv,
    u_send,
    u_recv,
    d_send,
    d_recv,
    t_send,
    t_recv,
    q_send,
    q_recv,
):
    tok = q_ref.shape[0]
    heads = lg_ref.shape[0]
    levels = lw_ref.shape[0]
    dk = q_ref.shape[1] // heads
    dv = v_ref.shape[1] // heads
    group = dk // dv
    pairs = heads // group
    spans = tok // SPAN
    span_bits = spans.bit_length() - 1
    bits = seq_count.bit_length() - 1
    half = heads // 2
    cross = [min(span_bits + 1 + b, levels - 1) for b in range(bits)]
    slots = sorted(set(cross))
    place = lax.axis_index("seq")
    row = lax.axis_index("head")
    bit = [(place // (1 << b)) % 2 for b in range(bits)]
    peer = [place + (1 - 2 * bit[b]) * (1 << b) for b in range(bits)]
    want_s = [(place // (2 << b)) != (seq_count // (2 << b)) - 1 for b in range(bits)]
    mine = bit[0] * half
    theirs = (1 - bit[0]) * half

    barrier = pltpu.get_barrier_semaphore()
    for o in range(1, seq_count):
        pl.semaphore_signal(
            barrier, inc=1, device_id={"seq": (place + o) % seq_count}, device_id_type=MESH
        )
    for o in range(1, head_count):
        pl.semaphore_signal(
            barrier, inc=1, device_id={"head": (row + o) % head_count}, device_id_type=MESH
        )

    rows_i = lax.broadcasted_iota(jnp.int32, (tok, tok), 0)
    cols_i = lax.broadcasted_iota(jnp.int32, (tok, tok), 1)
    tri = (rows_i <= cols_i).astype(F32)
    starts = jnp.broadcast_to(ds_ref[...].astype(F32), (8, tok))
    both = jnp.concatenate([lg_ref[...], starts], axis=0)
    cum_all = lax.dot_general(
        both, tri, NN, precision=lax.Precision.HIGHEST, preferred_element_type=F32
    )
    cum_t = jnp.transpose(cum_all)
    cum = cum_all[:heads]
    reset = cum_all[heads : heads + 1]
    reset_col = cum_t[:, heads : heads + 1]
    bias_s[...] = jnp.where((rows_i <= cols_i) & (reset == reset_col), 0.0, -1e30)
    end = cum[:, tok - 1 : tok]
    reset_end = reset[:, tok - 1 : tok]
    cum_s[...] = cum
    lead_s[...] = jnp.where(reset == 0, jnp.exp(cum), 0.0)
    tail_s[...] = jnp.where(reset == reset_end, jnp.exp(end - cum), 0.0)
    dec[0] = jnp.broadcast_to(jnp.where(reset_end == 0, jnp.exp(end), 0.0), (heads, dk))
    for h in range(heads):
        col_s[h] = jnp.broadcast_to(cum_t[:, h : h + 1], (tok, tok))

    def states(p, _):
        lanes = pl.ds(pl.multiple_of(p * dk, dk), dk)
        vt = jnp.transpose(v_ref[:, lanes].astype(F32))
        gt = jnp.transpose(g_ref[:, lanes].astype(F32))
        vt_s[p] = vt.astype(BF16)
        gt_s[p] = gt.astype(BF16)
        for i in range(group):
            h = p * group + i
            wide = pl.ds(pl.multiple_of(h * dk, dk), dk)
            part = slice(i * dv, (i + 1) * dv)
            tail = tail_s[pl.ds(h, 1), :]
            lead = lead_s[pl.ds(h, 1), :]
            state_s[h] = dot_fine(vt[part] * tail, k_ref[:, wide], NN)
            gw = jnp.concatenate(
                [gt[part] * (lead * lw_ref[l, pl.ds(h, 1), :]) for l in slots], axis=0
            )
            back = dot_fine(gw, q_ref[:, wide], NN)
            for n in range(len(slots)):
                back_s[n, h] = back[n * dv : (n + 1) * dv]
        return 0

    lax.fori_loop(0, pairs, states, 0)
    pl.semaphore_wait(barrier, seq_count - 1 + head_count - 1)

    def slot(b):
        return slots.index(cross[b])

    def remote(src, dst, send, recv, b):
        return pltpu.make_async_remote_copy(
            src_ref=src,
            dst_ref=dst,
            send_sem=send,
            recv_sem=recv,
            device_id={"seq": peer[b]},
            device_id_type=MESH,
        )

    own = pl.ds(mine, half)
    other = pl.ds(theirs, half)

    def u_copy(b, j):
        src = back_s.at[slot(j), other] if b == 0 else sum_u.at[b, j]
        return remote(src, got_u.at[b, j], u_send.at[b, j], u_recv.at[b, j], b)

    def s_copy(b):
        src = state_s.at[other] if b == 0 else sum_s.at[b]
        return remote(src, got_s.at[b], s_send.at[b], s_recv.at[b], b)

    def d_copy(b):
        return remote(dec.at[b], got_dec.at[b], d_send.at[b], d_recv.at[b], b)

    def level_copy(b, low):
        if b == 0:
            src = state_s if low else back_s.at[slot(0)]
            return [
                remote(src.at[part], lvl.at[0, part], lvl_send.at[0, n], lvl_recv.at[0, n], 0)
                for n, part in enumerate((other, own))
            ]
        src = sum_s.at[b] if low else sum_u.at[b, b]
        return [remote(src, lvl.at[b, own], lvl_send.at[b, 0], lvl_recv.at[b, 0], b)]

    def level_wait(b, n):
        part = other if n == 1 else own
        return remote(
            lvl.at[b, part], lvl.at[b, part], lvl_send.at[b, n], lvl_recv.at[b, n], b
        )

    def forward_copy(b, part):
        return remote(lvl.at[b, part], lvl.at[b, part], fwd_send.at[b], fwd_recv.at[b], 0)

    def begin(b):
        d_copy(b).start()

        @pl.when(bit[b] == 0)
        def _():
            for c in level_copy(b, True):
                c.start()

        if b < bits - 1:

            @pl.when((bit[b] == 1) & want_s[b])
            def _():
                s_copy(b).start()

            for j in range(b + 1, bits):

                @pl.when(bit[j] == 1)
                def _(j=j):
                    u_copy(b, j).start()

        @pl.when(bit[b] == 1)
        def _():
            for c in level_copy(b, False):
                c.start()

    def join(b):
        d_copy(b).wait_recv()
        level_wait(b, 0).wait_recv()
        if b > 0:
            forward_copy(b, own).start()
        up = bit[b].astype(F32)
        got = got_dec[b]
        now = dec[b]
        dec[b + 1] = got * now
        if b == bits - 1:
            return
        base_s = state_s.at[own] if b == 0 else sum_s.at[b]

        @pl.when(want_s[b])
        def _():
            @pl.when(bit[b] == 1)
            def _():
                def body(i, _):
                    d = dec[b, pl.ds(mine + i, 1), :]
                    sum_s[b + 1, i] = d * lvl[b, mine + i] + base_s[i]
                    return 0

                lax.fori_loop(0, half, body, 0, unroll=True)

            @pl.when(bit[b] == 0)
            def _():
                s_copy(b).wait_recv()

                def body(i, _):
                    d = got_dec[b, pl.ds(mine + i, 1), :]
                    sum_s[b + 1, i] = d * base_s[i] + got_s[b, i]
                    return 0

                lax.fori_loop(0, half, body, 0, unroll=True)

        for j in range(b + 1, bits):
            base_u = back_s.at[slot(j), own] if b == 0 else sum_u.at[b, j]

            @pl.when(bit[j] == 1)
            def _(j=j, base_u=base_u):
                u_copy(b, j).wait_recv()

                def body(i, _):
                    d0 = dec[b, pl.ds(mine + i, 1), :]
                    d1 = got_dec[b, pl.ds(mine + i, 1), :]
                    a = up * d1 + (1.0 - up)
                    c = (1.0 - up) * d0 + up
                    sum_u[b + 1, j, i] = a * base_u[i] + c * got_u[b, j, i]
                    return 0

                lax.fori_loop(0, half, body, 0, unroll=True)

    span_of = lax.broadcasted_iota(jnp.int32, (1, tok), 1) // SPAN

    def local(p, _):
        vt = vt_s[p]
        gt = gt_s[p]
        lanes = pl.ds(pl.multiple_of(p * dk, dk), dk)
        v_blk = v_ref[:, lanes]
        for i in range(group):
            h = p * group + i
            wide = pl.ds(pl.multiple_of(h * dk, dk), dk)
            part = slice(i * dv, (i + 1) * dv)
            q = q_ref[:, wide]
            k = k_ref[:, wide]
            score = dot(k, q, NT)
            pair = dot(v_blk[:, part], gt[part], NN)
            decay = jnp.exp((cum_s[pl.ds(h, 1), :] - col_s[h]) + bias_s[...])
            seen = decay * score
            both_p = seen * pair
            gains = [lw_ref[l, pl.ds(h, 1), :] for l in range(span_bits + 1)]
            level_rows = [jnp.zeros((1, tok), F32) for _ in range(span_bits + 1)]
            mixed, graded = [], []
            for cs in range(spans):
                rows = slice(cs * SPAN, (cs + 1) * SPAN)
                total = jnp.sum(both_p[rows], axis=0, keepdims=True)
                gain = jnp.zeros((1, tok), F32)
                for ct in range(cs, spans):
                    l = span_level(cs, ct, levels)
                    hit = span_of == ct
                    gain = jnp.where(hit, gains[l], gain)
                    level_rows[l] = level_rows[l] + jnp.where(hit, total, 0.0)
                mixed.append(seen[rows] * gain)
                graded.append(decay[rows] * gain * pair[rows])
            mix = jnp.concatenate(mixed, axis=0).astype(BF16)
            grade = jnp.concatenate(graded, axis=0).astype(BF16)
            for l in range(span_bits + 1):
                gl_ref[l, pl.ds(h, 1), :] = level_rows[l]
            drift_s[pl.ds(h, 1), :] = jnp.sum(mix.astype(F32) * pair, axis=0, keepdims=True)
            vg_s[p, part] = dot(gt[part], mix, NT)
            gk_s[h] = dot(grade, q, NN)
            gq_s[h] = dot(grade, k, TN)
        return 0

    begin(0)
    lax.fori_loop(0, pairs // 2, local, 0)
    join(0)
    if bits > 1:
        begin(1)
    lax.fori_loop(pairs // 2, pairs, local, 0)
    for b in range(1, bits):
        join(b)
        if b + 1 < bits:
            begin(b + 1)

    inner_f = jnp.ones((heads, dk), F32)
    inner_b = jnp.ones((heads, dk), F32)
    for b in range(bits):
        up = bit[b].astype(F32)
        got = got_dec[b]
        coef_s[0, b] = inner_f * up
        coef_s[1, b] = inner_b * (1.0 - up)
        inner_f = inner_f * (up * got + (1.0 - up))
        inner_b = inner_b * ((1.0 - up) * got + up)
    level_wait(0, 1).wait_recv()
    for b in range(1, bits):
        forward_copy(b, other).wait_recv()

    def finish(p, _):
        lanes = pl.ds(pl.multiple_of(p * dk, dk), dk)
        vt = vt_s[p].astype(F32)
        gt = gt_s[p].astype(F32)
        vg_all = []
        for i in range(group):
            h = p * group + i
            wide = pl.ds(pl.multiple_of(h * dk, dk), dk)
            part = slice(i * dv, (i + 1) * dv)
            q = q_ref[:, wide]
            k = k_ref[:, wide]
            tail = tail_s[pl.ds(h, 1), :]
            lead = lead_s[pl.ds(h, 1), :]
            blocks = [lvl[b, h] for b in range(bits)]
            entering = []
            for n in range(len(slots)):
                terms = [
                    coef_s[0, b, pl.ds(h, 1), :] * blocks[b] for b in range(bits) if slot(b) == n
                ]
                entering.append(functools.reduce(jnp.add, terms))
            entering = jnp.concatenate(entering, axis=0)
            after = functools.reduce(
                jnp.add, [coef_s[1, b, pl.ds(h, 1), :] * blocks[b] for b in range(bits)]
            )
            e_high, e_low = split(entering)
            seen = dot(e_high, q, NT) + dot(e_low, q, NT)
            drift = drift_s[pl.ds(h, 1), :]
            gws = []
            for n, l in enumerate(slots):
                gain = lw_ref[l, pl.ds(h, 1), :]
                level = lead * jnp.sum(
                    seen[n * dv : (n + 1) * dv] * gt[part], axis=0, keepdims=True
                )
                gl_ref[l, pl.ds(h, 1), :] = level
                drift = drift + gain * level
                gws.append(gt[part] * (lead * gain))
            gw, gw_low = split(jnp.concatenate(gws, axis=0))
            gq_in = dot(gw, e_high, TN) + dot(gw, e_low, TN) + dot(gw_low, e_high, TN)
            gq_ref[:, wide] = (gq_s[h] + gq_in).astype(BF16)
            a_high, a_low = split(after)
            tv, tv_low = split(vt[part] * tail)
            gk_in = dot(tv, a_high, TN) + dot(tv, a_low, TN) + dot(tv_low, a_high, TN)
            gk_ref[:, wide] = (gk_s[h] + gk_in).astype(BF16)
            vg = vg_s[p, part] + tail * (dot(a_high, k, NT) + dot(a_low, k, NT))
            drift_s[pl.ds(h, 1), :] = drift - jnp.sum(vg * vt[part], axis=0, keepdims=True)
            vg_all.append(vg)
        gv_ref[:, lanes] = jnp.transpose(jnp.concatenate(vg_all, axis=0)).astype(BF16)
        return 0

    lax.fori_loop(0, pairs, finish, 0)
    for l in range(levels):
        if l > span_bits and l not in slots:
            gl_ref[l] = jnp.zeros((heads, tok), F32)

    later = (rows_i >= cols_i).astype(F32)
    local_tail = lax.dot_general(
        drift_s[...], later, NN, precision=lax.Precision.HIGHEST, preferred_element_type=F32
    )
    lane = lax.broadcasted_iota(jnp.int32, (heads, tok), 1)
    first = local_tail[:, 0:1]
    plain = jnp.sum(local_tail, axis=1, keepdims=True)
    square = jnp.sum(local_tail * local_tail, axis=1, keepdims=True)
    tot[place] = jnp.where(lane == 0, first, jnp.where(lane == 1, plain, square))

    def tot_copy(o, slot_at):
        return pltpu.make_async_remote_copy(
            src_ref=tot.at[place],
            dst_ref=tot.at[slot_at],
            send_sem=t_send.at[o],
            recv_sem=t_recv.at[slot_at],
            device_id={"seq": (place + o) % seq_count},
            device_id_type=MESH,
        )

    for o in range(1, seq_count):
        tot_copy(o, place).start()
    for o in range(1, seq_count):
        tot_copy(o, (place + o) % seq_count).wait_recv()
    after_total = jnp.zeros((heads, 1), F32)
    my_later = jnp.zeros((heads, 1), F32)
    energy = jnp.zeros((heads, 1), F32)
    for d in reversed(range(seq_count)):
        piece = tot[d]
        my_later = my_later + jnp.where(place == d, 1.0, 0.0) * after_total
        energy = energy + (
            piece[:, 2:3] + after_total * (2.0 * piece[:, 1:2] + tok * after_total)
        )
        after_total = after_total + piece[:, 0:1]
    energy = jnp.sum(jnp.broadcast_to(energy, (heads, dk)), axis=0, keepdims=True)
    sq[row] = jnp.broadcast_to(energy, (8, dk))

    def sq_copy(o, slot_at):
        return pltpu.make_async_remote_copy(
            src_ref=sq.at[row],
            dst_ref=sq.at[slot_at],
            send_sem=q_send.at[o],
            recv_sem=q_recv.at[slot_at],
            device_id={"head": (row + o) % head_count},
            device_id_type=MESH,
        )

    for o in range(1, head_count):
        sq_copy(o, row).start()
    for o in range(1, head_count):
        sq_copy(o, (row + o) % head_count).wait_recv()
    whole = sq[0]
    for r in range(1, head_count):
        whole = whole + sq[r]
    count = heads * tok * seq_count * head_count
    factor = jnp.minimum(1.0, lax.rsqrt(whole[0:1] / count + 1e-6))
    gg_ref[...] = (local_tail + my_later) * factor

    for b in range(bits):
        d_copy(b).wait_send()
        for n in range(2 if b == 0 else 1):
            level_wait(b, n).wait_send()
        if b > 0:
            forward_copy(b, own).wait_send()
        if b < bits - 1:

            @pl.when((bit[b] == 1) & want_s[b])
            def _(b=b):
                s_copy(b).wait_send()

            for j in range(b + 1, bits):

                @pl.when(bit[j] == 1)
                def _(b=b, j=j):
                    u_copy(b, j).wait_send()

    for o in range(1, seq_count):
        tot_copy(o, place).wait_send()
    for o in range(1, head_count):
        sq_copy(o, row).wait_send()


def shards(seq_count, head_count, queries, keys, values, out_grad, log_gate, level_weight, doc_start):
    tok = queries.shape[0]
    heads = log_gate.shape[0]
    levels = level_weight.shape[0]
    dk = queries.shape[1] // heads
    dv = values.shape[1] // heads
    group = dk // dv
    pairs = heads // group
    bits = seq_count.bit_length() - 1
    half = heads // 2
    span_bits = (tok // SPAN).bit_length() - 1
    slots = len({min(span_bits + 1 + b, levels - 1) for b in range(bits)})
    dma = pltpu.SemaphoreType.DMA
    vmem = pltpu.VMEM
    block = (dv, dk)
    scratch = [
        vmem((heads, tok), F32),
        vmem((heads, tok, tok), F32),
        vmem((heads, tok), F32),
        vmem((heads, tok), F32),
        vmem((tok, tok), F32),
        vmem((pairs, group * dv, tok), BF16),
        vmem((pairs, group * dv, tok), BF16),
        vmem((pairs, group * dv, tok), F32),
        vmem((heads, tok, dk), F32),
        vmem((heads, tok, dk), F32),
        vmem((heads, tok), F32),
        vmem((2, bits, heads, dk), F32),
        vmem((heads,) + block, F32),
        vmem((slots, heads) + block, F32),
        vmem((bits, heads) + block, F32),
        vmem((bits, half) + block, F32),
        vmem((bits, bits, half) + block, F32),
        vmem((bits, half) + block, F32),
        vmem((bits, bits, half) + block, F32),
        vmem((bits + 1, heads, dk), F32),
        vmem((bits, heads, dk), F32),
        vmem((seq_count, heads, tok), F32),
        vmem((head_count, 8, dk), F32),
        dma((bits, 2)),
        dma((bits, 2)),
        dma((bits,)),
        dma((bits,)),
        dma((bits,)),
        dma((bits,)),
        dma((bits, bits)),
        dma((bits, bits)),
        dma((bits,)),
        dma((bits,)),
        dma((seq_count,)),
        dma((seq_count,)),
        dma((head_count,)),
        dma((head_count,)),
    ]
    spec = pl.BlockSpec(memory_space=pltpu.VMEM)
    return pl.pallas_call(
        functools.partial(kernel, seq_count, head_count),
        out_shape=(
            jax.ShapeDtypeStruct(queries.shape, BF16),
            jax.ShapeDtypeStruct(keys.shape, BF16),
            jax.ShapeDtypeStruct(values.shape, BF16),
            jax.ShapeDtypeStruct(level_weight.shape, F32),
            jax.ShapeDtypeStruct(log_gate.shape, F32),
        ),
        in_specs=[spec] * 7,
        out_specs=(spec,) * 5,
        scratch_shapes=scratch,
        compiler_params=pltpu.CompilerParams(collective_id=0, has_side_effects=True),
    )(queries, keys, values, out_grad, log_gate, level_weight, doc_start.reshape(1, tok))


def solution(mesh):
    return jax.shard_map(
        functools.partial(shards, mesh.shape["seq"], mesh.shape["head"]),
        mesh=mesh,
        in_specs=(
            P("seq", "head"),
            P("seq", "head"),
            P("seq", "head"),
            P("seq", "head"),
            P("head", "seq"),
            P(None, "head", "seq"),
            P("seq"),
        ),
        out_specs=(
            P("seq", "head"),
            P("seq", "head"),
            P("seq", "head"),
            P(None, "head", "seq"),
            P("head", "seq"),
        ),
        check_vma=False,
    )
```

profile of v0, /device:TPU:0, one launch (start us, length us, event | category | flops | bytes accessed | tf_op | source)
XLA Modules:
  0.0 50.7 jit_solution(9861559671453997818)
XLA Ops:
  0.6 44.9 %shard_map.110 = (bf16[128,2048]{1,0:T(8,128)(2,1)}, bf16[128,2048]{1,0:T(8,128)(2,1)}, bf16[128,1024]{1,0:T(8,128)(2,1)}, f32[6,16,128]{2,1,0:T(8,128)}, f32[16,128]{1,0:T(8,128)}) custom-call(bf16[128,2048]{1,0:T(8,128)(2,1)} %q_ref.1, bf16[128,2048]{1,0:T(8,128)(2,1)} %k_ref.1, bf16[128,1024]{1,0:T(8,128)(2,1)} %v_ref.1, bf16[128,1024]{1,0:T(8,128)(2,1)} %g_ref.1, ...), custom_call_target="tpu_custom_call" | custom-call | tf_op jit(solution)/shard_map/pallas_call | solution.py:547
  45.6 0.0 copy-start
  45.6 1.9 %copy.17 = bf16[128,2048]{1,0:T(8,128)(2,1)} copy(bf16[128,2048]{1,0:T(8,128)(2,1)} %get-tuple-element.10) | data formatting | bytes 1048576
  47.5 0.0 copy-done
  47.5 0.0 copy-start.1
  47.5 0.8 %copy.18 = bf16[128,2048]{1,0:T(8,128)(2,1)} copy(bf16[128,2048]{1,0:T(8,128)(2,1)S(1)} %copy-done) | data formatting | bytes 1048576
  48.3 0.3 copy-done.1
  48.6 0.0 copy-start.2
  48.6 0.7 %copy.19 = bf16[128,1024]{1,0:T(8,128)(2,1)} copy(bf16[128,1024]{1,0:T(8,128)(2,1)S(1)} %copy-done.1) | data formatting | bytes 524288
  49.3 0.1 copy-done.2
  49.4 0.0 copy-start.3
  49.4 0.6 %copy.20 = f32[6,16,128]{2,1,0:T(8,128)} copy(f32[6,16,128]{2,1,0:T(8,128)S(1)} %copy-done.2) | data formatting | bytes 98304
  50.0 0.1 copy-done.3
  50.1 0.6 %copy.21 = f32[16,128]{1,0:T(8,128)} copy(f32[16,128]{1,0:T(8,128)S(1)} %copy-done.3) | data formatting | bytes 16384
Async XLA Ops:
  45.6 2.0 %copy-start = (bf16[128,2048]{1,0:T(8,128)(2,1)S(1)}, bf16[128,2048]{1,0:T(8,128)(2,1)}, u32[]{:S(2)}) copy-start(bf16[128,2048]{1,0:T(8,128)(2,1)} %get-tuple-element.11) | copy-start | bytes 1572868
  47.5 1.1 %copy-start.1 = (bf16[128,1024]{1,0:T(8,128)(2,1)S(1)}, bf16[128,1024]{1,0:T(8,128)(2,1)}, u32[]{:S(2)}) copy-start(bf16[128,1024]{1,0:T(8,128)(2,1)} %get-tuple-element.12) | copy-start | bytes 786436
  48.6 0.8 %copy-start.2 = (f32[6,16,128]{2,1,0:T(8,128)S(1)}, f32[6,16,128]{2,1,0:T(8,128)}, u32[]{:S(2)}) copy-start(f32[6,16,128]{2,1,0:T(8,128)} %get-tuple-element.13) | copy-start | bytes 147460
  49.4 0.7 %copy-start.3 = (f32[16,128]{1,0:T(8,128)S(1)}, f32[16,128]{1,0:T(8,128)}, u32[]{:S(2)}) copy-start(f32[16,128]{1,0:T(8,128)} %get-tuple-element.14) | copy-start | bytes 24580
where the time goes:
time: 51 us; the launch traced here: 50.7 us
  Pallas kernels  44.9 us (88%)
  local copies, waits for them, and re-layouts  5.13 us (10%)
  between operations  0.66 us (1%)
    pallas_call x1, Pallas kernels, shards(): pl.pallas_call(functools.partial(kernel, seq_count, head_count), out_shap...  44.9 us
    unnamed x13, local copies, waits for them, and re-layouts  5.13 us

commit v1 on v0

--- a/solution.py
+++ b/solution.py
@@ -161,7 +161,7 @@
                 back_s[n, h] = back[n * dv : (n + 1) * dv]
         return 0
 
-    lax.fori_loop(0, pairs, states, 0)
+    lax.fori_loop(0, pairs, states, 0, unroll=2)
     pl.semaphore_wait(barrier, seq_count - 1 + head_count - 1)
 
     def slot(b):
@@ -210,10 +210,22 @@
     def forward_copy(b, part):
         return remote(lvl.at[b, part], lvl.at[b, part], fwd_send.at[b], fwd_recv.at[b], 0)
 
+    def land(b):
+        up_summed = (bit[b] == 1) & want_s[b]
+
+        @pl.when(jnp.logical_not(up_summed))
+        def _():
+            level_wait(b, 0).wait_recv()
+
+        if b > 0:
+            forward_copy(b, own).start()
+
     def begin(b):
         d_copy(b).start()
 
-        @pl.when(bit[b] == 0)
+        early = 0 if b in (0, bits - 1) else 1
+
+        @pl.when((bit[b] == 0) & (want_s[b] | (early == 0)))
         def _():
             for c in level_copy(b, True):
                 c.start()
@@ -229,6 +241,22 @@
                 @pl.when(bit[j] == 1)
                 def _(j=j):
                     u_copy(b, j).start()
+
+        if early == 0:
+
+            @pl.when(bit[b] == 1)
+            def _():
+                for c in level_copy(b, False):
+                    c.start()
+
+    def begin_late(b):
+        if b in (0, bits - 1):
+            return
+
+        @pl.when((bit[b] == 0) & jnp.logical_not(want_s[b]))
+        def _():
+            for c in level_copy(b, True):
+                c.start()
 
         @pl.when(bit[b] == 1)
         def _():
@@ -237,9 +265,6 @@
 
     def join(b):
         d_copy(b).wait_recv()
-        level_wait(b, 0).wait_recv()
-        if b > 0:
-            forward_copy(b, own).start()
         up = bit[b].astype(F32)
         got = got_dec[b]
         now = dec[b]
@@ -252,6 +277,8 @@
         def _():
             @pl.when(bit[b] == 1)
             def _():
+                level_wait(b, 0).wait_recv()
+
                 def body(i, _):
                     d = dec[b, pl.ds(mine + i, 1), :]
                     sum_s[b + 1, i] = d * lvl[b, mine + i] + base_s[i]
@@ -330,15 +357,18 @@
         return 0
 
     begin(0)
-    lax.fori_loop(0, pairs // 2, local, 0)
+    lax.fori_loop(0, pairs // 4, local, 0, unroll=2)
     join(0)
     if bits > 1:
         begin(1)
-    lax.fori_loop(pairs // 2, pairs, local, 0)
+    lax.fori_loop(pairs // 4, pairs, local, 0, unroll=2)
     for b in range(1, bits):
         join(b)
         if b + 1 < bits:
             begin(b + 1)
+        begin_late(b)
+        land(b - 1)
+    land(bits - 1)
 
     inner_f = jnp.ones((heads, dk), F32)
     inner_b = jnp.ones((heads, dk), F32)
@@ -402,7 +432,7 @@
         gv_ref[:, lanes] = jnp.transpose(jnp.concatenate(vg_all, axis=0)).astype(BF16)
         return 0
 
-    lax.fori_loop(0, pairs, finish, 0)
+    lax.fori_loop(0, pairs, finish, 0, unroll=2)
     for l in range(levels):
         if l > span_bits and l not in slots:
             gl_ref[l] = jnp.zeros((heads, tok), F32)

time: 51 us -> 44.9 us (0.88)
  Pallas kernels: 44.9 us -> 38.9 us
    pallas_call x1, Pallas kernels: 44.9 us -> 38.9 us  [shards(): pl.pallas_call(functools.partial(kernel, seq_count, head_count), out_shap...]
where the time goes in v1:
time: 44.9 us; the launch traced here: 44.6 us
  Pallas kernels  38.9 us (87%)
  local copies, waits for them, and re-layouts  5.13 us (11%)
  between operations  0.66 us (1%)
    pallas_call x1, Pallas kernels, shards(): pl.pallas_call(functools.partial(kernel, seq_count, head_count), out_shap...  38.9 us
    unnamed x13, local copies, waits for them, and re-layouts  5.13 us

profile of v1, /device:TPU:0, one launch (start us, length us, event | category | flops | bytes accessed | tf_op | source)
XLA Modules:
  0.0 44.6 jit_solution(12261945428217930794)
XLA Ops:
  0.6 38.9 %shard_map.110 = (bf16[128,2048]{1,0:T(8,128)(2,1)}, bf16[128,2048]{1,0:T(8,128)(2,1)}, bf16[128,1024]{1,0:T(8,128)(2,1)}, f32[6,16,128]{2,1,0:T(8,128)}, f32[16,128]{1,0:T(8,128)}) custom-call(bf16[128,2048]{1,0:T(8,128)(2,1)} %q_ref.1, bf16[128,2048]{1,0:T(8,128)(2,1)} %k_ref.1, bf16[128,1024]{1,0:T(8,128)(2,1)} %v_ref.1, bf16[128,1024]{1,0:T(8,128)(2,1)} %g_ref.1, ...), custom_call_target="tpu_custom_call" | custom-call | tf_op jit(solution)/shard_map/pallas_call | solution.py:577
  39.5 0.0 copy-start
  39.5 1.9 %copy.17 = bf16[128,2048]{1,0:T(8,128)(2,1)} copy(bf16[128,2048]{1,0:T(8,128)(2,1)} %get-tuple-element.10) | data formatting | bytes 1048576
  41.4 0.0 copy-done
  41.5 0.0 copy-start.1
  41.5 0.8 %copy.18 = bf16[128,2048]{1,0:T(8,128)(2,1)} copy(bf16[128,2048]{1,0:T(8,128)(2,1)S(1)} %copy-done) | data formatting | bytes 1048576
  42.2 0.3 copy-done.1
  42.5 0.0 copy-start.2
  42.5 0.7 %copy.19 = bf16[128,1024]{1,0:T(8,128)(2,1)} copy(bf16[128,1024]{1,0:T(8,128)(2,1)S(1)} %copy-done.1) | data formatting | bytes 524288
  43.2 0.1 copy-done.2
  43.3 0.0 copy-start.3
  43.3 0.6 %copy.20 = f32[6,16,128]{2,1,0:T(8,128)} copy(f32[6,16,128]{2,1,0:T(8,128)S(1)} %copy-done.2) | data formatting | bytes 98304
  44.0 0.1 copy-done.3
  44.0 0.6 %copy.21 = f32[16,128]{1,0:T(8,128)} copy(f32[16,128]{1,0:T(8,128)S(1)} %copy-done.3) | data formatting | bytes 16384
Async XLA Ops:
  39.5 2.0 %copy-start = (bf16[128,2048]{1,0:T(8,128)(2,1)S(1)}, bf16[128,2048]{1,0:T(8,128)(2,1)}, u32[]{:S(2)}) copy-start(bf16[128,2048]{1,0:T(8,128)(2,1)} %get-tuple-element.11) | copy-start | bytes 1572868
  41.5 1.1 %copy-start.1 = (bf16[128,1024]{1,0:T(8,128)(2,1)S(1)}, bf16[128,1024]{1,0:T(8,128)(2,1)}, u32[]{:S(2)}) copy-start(bf16[128,1024]{1,0:T(8,128)(2,1)} %get-tuple-element.12) | copy-start | bytes 786436
  42.5 0.8 %copy-start.2 = (f32[6,16,128]{2,1,0:T(8,128)S(1)}, f32[6,16,128]{2,1,0:T(8,128)}, u32[]{:S(2)}) copy-start(f32[6,16,128]{2,1,0:T(8,128)} %get-tuple-element.13) | copy-start | bytes 147460
  43.3 0.7 %copy-start.3 = (f32[16,128]{1,0:T(8,128)S(1)}, f32[16,128]{1,0:T(8,128)}, u32[]{:S(2)}) copy-start(f32[16,128]{1,0:T(8,128)} %get-tuple-element.14) | copy-start | bytes 24580
